TPU v7x, 32 devices: a whole 2x2x4 slice. The times are simulated.
32 devices in a mesh: gy: 16 (over z, y, core), gz: 2 (over x).
Axes of the slice: x: 2, y: 2, z: 4, core: 2. Of those that a mesh axis runs over, the one named last changes fastest.
Arguments:
- scalar: float32 [8, 384, 384], P('gz', 'gy'), may hold values from -6 to 6
- velocity: float32 [3, 8, 128, 128], P(None, None, 'gy', 'gz'), may hold values from -0.9 to 0.9
Outputs:
- remeshed: float32 [8, 384, 384], P('gz', 'gy')
All inputs are finite; a program needn't handle non-finite values.
Results may differ from a plain program's by a relative error of at most 0.0003.
Values sent between devices are 32-bit elements; how exact they have to be, the bound alone decides.
A program may use at most 64 MiB of HBM per device.

v0:
```python
import jax
import jax.numpy as jnp
from jax import lax
from jax.sharding import PartitionSpec as P


def padded_2(value, sides, width):
    for axis, dim in sides:
        peers, length = (lax.axis_size(axis), value.shape[dim])
        up = [(i, (i + 1) % peers) for i in range(peers - 1)]
        down = [(j, i) for i, j in up]
        last = lax.slice_in_dim(value, length - width, length, axis=dim)
        initial = lax.slice_in_dim(value, 0, width, axis=dim)
        before = lax.ppermute(last, axis, up)
        after = lax.ppermute(initial, axis, down)
        value = jnp.concatenate([before, value, after], axis=dim)
    return value


def passed_along(block, axis, distance):
    devices = range(lax.axis_size(axis))
    route = [((i - distance) % len(devices), i) for i in devices]
    return lax.ppermute(block, axis, route)


def alternate(current, following, along):
    pieces = [current * (1.0 - phase / 3.0) + following * (phase / 3.0) for phase in range(3)]
    stacked = jnp.stack(pieces, axis=along + 1)
    new_shape = list(current.shape)
    new_shape[along] = new_shape[along] * 3
    return stacked.reshape(new_shape)


def polynomial(factors, value):
    result = jnp.zeros_like(value)
    for factor in reversed(factors):
        result = result * value + factor
    return result


def kernel_weight(offset):
    size = jnp.abs(offset)
    inner = polynomial([1.0, 0.0, -5.0 / 4.0, -35.0 / 12.0, 21.0 / 4.0, -25.0 / 12.0], size)
    middle = polynomial(
        [-4.0, 75.0 / 4.0, -245.0 / 8.0, 545.0 / 24.0, -63.0 / 8.0, 25.0 / 24.0], size
    )
    outer = polynomial(
        [18.0, -153.0 / 4.0, 255.0 / 8.0, -313.0 / 24.0, 21.0 / 8.0, -5.0 / 24.0], size
    )
    return jnp.where(
        size < 1.0, inner, jnp.where(size < 2.0, middle, jnp.where(size < 3.0, outer, 0.0))
    )


def displacement(speed, before, after):
    half_step = 0.5 * speed
    return jnp.where(
        half_step >= 0.0,
        (1.0 - half_step) * speed + half_step * after,
        (1.0 + half_step) * speed - half_step * before,
    )


def sweep_periodic(field, speed, along):
    moved = displacement(speed, jnp.roll(speed, 1, along), jnp.roll(speed, -1, along))
    result = jnp.zeros_like(field)
    for offset in range(-3, 4):
        result = result + jnp.roll(field * kernel_weight(offset - moved), offset, along)
    return result


def sweep_open(field, speed, padded):
    padded = padded_2(speed, (("gz", 0),), 1)
    moved = displacement(speed, padded[:-2], padded[2:])
    count = field.shape[0]
    total = jnp.zeros((count + 6,) + field.shape[1:], jnp.float32)
    for offset in range(-3, 4):
        total = total.at[3 + offset : 3 + offset + count].add(field * kernel_weight(offset - moved))
    ghosts = jnp.concatenate([total[:3], total[count + 3 :]], axis=0)
    received = padded_2(ghosts, (("gz", 0),), 3)
    result = total[3 : count + 3]
    result = result.at[:3].add(received[:3])
    result = result.at[count - 3 :].add(received[9:])
    return result


def local(scalar, velocity):
    coarse = lax.all_to_all(velocity, "gz", split_axis=1, concat_axis=3, tiled=True)
    rows_part = coarse[:1]
    next_row = passed_along(rows_part[:, :, :1, :], "gy", -1)
    y_fine = alternate(rows_part, jnp.concatenate([rows_part[:, :, 1:, :], next_row], axis=2), 2)
    fine_vel = alternate(y_fine, jnp.roll(y_fine, -1, 3), 3)
    field = sweep_periodic(scalar, fine_vel[0], 2)
    turned = jnp.swapaxes(field, 1, 2)
    padded_z = None
    sending = coarse[1:]
    field = lax.all_to_all(turned, "gy", split_axis=1, concat_axis=2, tiled=True)
    coarse_rows = jnp.swapaxes(sending, 2, 3)
    coarse_turned = lax.all_to_all(coarse_rows, "gy", split_axis=2, concat_axis=3, tiled=True)
    y_refined = alternate(coarse_turned, jnp.roll(coarse_turned, -1, 3), 3)
    next_col = passed_along(y_refined[:, :, :1, :], "gy", -1)
    pencil_vel = alternate(
        y_refined, jnp.concatenate([y_refined[:, :, 1:, :], next_col], axis=2), 2
    )
    speed_y = pencil_vel[0]
    speed_z = pencil_vel[1]
    field = sweep_periodic(field, speed_y, 2)
    return sweep_open(field, speed_z, padded_z)


def solution(mesh):
    in_specs = (P("gz", "gy", None), P(None, None, "gy", "gz"))
    out_specs = P("gz", "gy", None)
    return jax.shard_map(local, mesh=mesh, in_specs=in_specs, out_specs=out_specs, check_vma=False)
```

profile of v0, /device:TPU:0, one launch (start us, length us, event | category | flops | bytes accessed | tf_op | source)
XLA Modules:
  0.0 67.6 jit_solution(13665253573162339864)
XLA Ops:
  0.0 0.9 %copy.405 = f32[3,8,8,64]{3,2,0,1:T(8,128)S(1)} copy(f32[3,8,8,64]{3,2,1,0:T(8,128)} %param.21) | data formatting | bytes 98304 | tf_op args[1]
  1.0 8.1 %all_to_all.54 = f32[2,1,6144]{2,1,0:T(1,128)S(1)} all-to-all(f32[2,1,6144]{2,1,0:T(1,128)S(1)} %reshape.847), channel_id=1, replica_groups=mesh['gy'=16,'gz'=2] {'gz'}, dimensions={0} | all-to-all | bytes 98304 | tf_op jit(solution)/shard_map/all_to_all | solution.py:88
  9.1 0.5 broadcast.909
  9.6 0.8 %reduce.18 = f32[2,6144]{1,0:T(2,128)S(1)} reduce(f32[2,1,6144]{2,1,0:T(1,128)S(1)} %all_to_all.54, f32[]{:T(128)} %broadcast.909), dimensions={1}, to_apply=%all_to_all.39.reduce_sub_computation | reduce | bytes 98308 | tf_op jit(solution)/shard_map/all_to_all | solution.py:88
  10.7 2.7 %collective-permute-start = (f32[1,4,1,128]{3,2,1,0:T(1,128)S(1)}, f32[1,4,1,128]{3,2,1,0:T(1,128)S(1)}, u32[]{:S(2)}, u32[]{:S(2)}) collective-permute-start(f32[1,4,1,128]{3,2,1,0:T(1,128)S(1)} %slice.470), channel_id=1, source_target_pairs={{2,0},{4,2},{6,4},{8,6},{10,8},{12,10},{14,12},{16,14},{18,16},{20... | collective-permute-start | bytes 6152 | tf_op jit(solution)/shard_map/ppermute | solution.py:23
  13.8 1.1 %reshape.851 = f32[16,1,512]{2,1,0:T(1,128)} reshape(f32[128,2,4,8]{3,2,1,0:T(4,128)S(1)} %bitcast.81) | data formatting | bytes 65536
  15.0 3.5 %all-to-all-start.2 = ((f32[16,1,512]{2,1,0:T(1,128)}), f32[16,1,512]{2,1,0:T(1,128)S(1)}, u32[]{:S(2)}, u32[]{:S(2)}) async-start(f32[16,1,512]{2,1,0:T(1,128)} %reshape.851), calls=%async_computation.2 | async-start | bytes 65536 | tf_op jit(solution)/shard_map/all_to_all | solution.py:99
  20.2 1.0 %fusion.22 = (f32[4,24,384]{2,1,0:T(8,128)S(1)}, f32[4,24,384]{2,1,0:T(8,128)S(1)}, f32[4,24,384]{2,1,0:T(8,128)S(1)}, f32[4,24,384]{2,1,0:T(8,128)S(1)}, f32[4,24,384]{2,1,0:T(8,128)S(1)}) fusion(f32[4,24,384]{2,1,0:T(8,128)S(1)} %copy-done, f32[4,24,384]{2,1,0:T(8,128)S(1)} %get-tuple-element.121), kind=kLoop, calls=%fused_computation.47 | loop fusion | flops 7741440 | bytes 1032192 | tf_op jit(solution)/shard_map/mul | solution.py:68
  22.4 1.7 %reshape.849 = f32[16,1,2304]{2,1,0:T(1,128)} reshape(f32[384,4,24]{2,1,0:T(4,128)S(1)} %bitcast.78) | data formatting | bytes 294912
  24.1 1.0 %all-to-all-done.2 = f32[16,1,512]{2,1,0:T(1,128)S(1)} async-done(((f32[16,1,512]{2,1,0:T(1,128)}), f32[16,1,512]{2,1,0:T(1,128)S(1)}, u32[]{:S(2)}, u32[]{:S(2)}) %all-to-all-start.2) | async-done | bytes 32800 | tf_op jit(solution)/shard_map/all_to_all | solution.py:99
  25.1 4.9 %all-to-all-start.1 = ((f32[16,1,2304]{2,1,0:T(1,128)}), f32[16,1,2304]{2,1,0:T(1,128)S(1)}, u32[]{:S(2)}, u32[]{:S(2)}) async-start(f32[16,1,2304]{2,1,0:T(1,128)} %reshape.849), calls=%async_computation.1 | async-start | bytes 294912 | tf_op jit(solution)/shard_map/all_to_all | solution.py:97
  30.0 0.7 %reduce.19 = f32[16,512]{1,0:T(8,128)S(1)} reduce(f32[16,1,512]{2,1,0:T(1,128)S(1)} %all-to-all-done.2, f32[]{:T(128)} %broadcast.909), dimensions={1}, to_apply=%all_to_all.46.reduce_sub_computation | reduce | bytes 65540 | tf_op jit(solution)/shard_map/all_to_all | solution.py:99
  30.8 0.6 reshape.852
  32.4 0.7 %copy.364 = f32[2,4,8,128,3]{2,1,4,3,0:T(4,128)S(1)} copy(f32[2,4,8,128,3]{3,2,1,0,4:T(8,128)S(1)} %pad_maximum_fusion.4) | data formatting | bytes 196608 | tf_op jit(solution)/shard_map/stack | solution.py:28
  33.1 0.6 copy.366
  33.8 4.4 %collective-permute-start.1 = (f32[2,4,1,384]{3,1,2,0:T(4,128)S(1)}, f32[2,4,1,384]{3,1,2,0:T(4,128)S(1)}, u32[]{:S(2)}, u32[]{:S(2)}) collective-permute-start(f32[2,4,1,384]{3,1,2,0:T(4,128)S(1)} %copy.366), channel_id=1, source_target_pairs={{2,0},{4,2},{6,4},{8,6},{10,8},{12,10},{14,12},{16,14},{18,16},{20... | collective-permute-start | bytes 36872 | tf_op jit(solution)/shard_map/ppermute | solution.py:23
  38.2 0.9 %slice_bitcast_fusion = f32[2,4,7,1,384]{2,1,4,0,3:T(4,128)S(1)} fusion(f32[2,4,8,384]{2,1,3,0:T(4,128)S(1)} %bitcast.70), kind=kLoop, calls=%fused_computation | loop fusion | bytes 172032 | tf_op jit(solution)/shard_map/concatenate | solution.py:103
  39.1 0.6 copy.369
  39.6 0.7 copy.367
  40.5 2.2 %collective-permute-start.3 = (f32[1,24,384]{2,0,1:T(1,128)S(1)}, f32[1,24,384]{2,0,1:T(1,128)S(1)}, u32[]{:S(2)}, u32[]{:S(2)}) collective-permute-start(f32[1,24,384]{2,0,1:T(1,128)S(1)} %bitcast.97), channel_id=1, source_target_pairs={{0,1},{2,3},{4,5},{6,7},{8,9},{10,11},{12,13},{14,15},{16,17},{18,... | collective-permute-start | bytes 110600 | tf_op jit(solution)/shard_map/ppermute | solution.py:14
  42.8 1.5 %collective-permute-start.2 = (f32[1,24,384]{2,0,1:T(1,128)S(1)}, f32[1,24,384]{2,0,1:T(1,128)S(1)}, u32[]{:S(2)}, u32[]{:S(2)}) collective-permute-start(f32[1,24,384]{2,0,1:T(1,128)S(1)} %bitcast.98), channel_id=1, source_target_pairs={{1,0},{3,2},{5,4},{7,6},{9,8},{11,10},{13,12},{15,14},{17,16},{19,... | collective-permute-start | bytes 110600 | tf_op jit(solution)/shard_map/ppermute | solution.py:15
  44.7 3.9 %collective-permute-done.2 = f32[1,24,384]{2,0,1:T(1,128)S(1)} collective-permute-done((f32[1,24,384]{2,0,1:T(1,128)S(1)}, f32[1,24,384]{2,0,1:T(1,128)S(1)}, u32[]{:S(2)}, u32[]{:S(2)}) %collective-permute-start.2) | collective-permute-done | bytes 36896 | tf_op jit(solution)/shard_map/ppermute | solution.py:15
  48.6 1.0 %reduce.20 = f32[16,2304]{1,0:T(8,128)S(1)} reduce(f32[16,1,2304]{2,1,0:T(1,128)S(1)} %all-to-all-done.1, f32[]{:T(128)} %broadcast.909), dimensions={1}, to_apply=%all_to_all.42.reduce_sub_computation | reduce | bytes 294916 | tf_op jit(solution)/shard_map/all_to_all | solution.py:97
  49.6 1.1 %reshape.850 = f32[384,4,24]{2,1,0:T(4,128)S(1)} reshape(f32[16,2304]{1,0:T(8,128)S(1)} %reduce.20) | data formatting | bytes 294912
  50.7 0.5 copy.402
  51.9 1.0 %fusion.28 = (f32[4,24,384]{2,1,0:T(8,128)S(1)}, f32[4,24,384]{2,1,0:T(8,128)S(1)}, f32[4,24,384]{2,1,0:T(8,128)S(1)}, f32[4,24,384]{2,1,0:T(8,128)S(1)}, f32[4,24,384]{2,1,0:T(8,128)S(1)}) fusion(f32[4,24,384]{2,1,0:T(8,128)S(1)} %all_to_all.45, f32[4,24,384]{2,1,0:T(8,128)S(1)} %get-tuple-element.119), kind=kLoop, calls=%fused_computation.53 | loop fusion | flops 7741440 | bytes 1032192 | tf_op jit(solution)/shard_map/mul | solution.py:68
  53.5 0.6 fusion.53
  55.4 1.6 %collective-permute-start.4 = (f32[3,24,384]{2,1,0:T(8,128)S(1)}, f32[3,24,384]{2,1,0:T(8,128)S(1)}, u32[]{:S(2)}, u32[]{:S(2)}) collective-permute-start(f32[3,24,384]{2,1,0:T(8,128)S(1)} %slice.519), channel_id=1, source_target_pairs={{0,1},{2,3},{4,5},{6,7},{8,9},{10,11},{12,13},{14,15},{16,17},{18,... | collective-permute-start | bytes 331784 | tf_op jit(solution)/shard_map/ppermute | solution.py:14
  57.1 2.3 %collective-permute-done.4 = f32[3,24,384]{2,1,0:T(8,128)S(1)} collective-permute-done((f32[3,24,384]{2,1,0:T(8,128)S(1)}, f32[3,24,384]{2,1,0:T(8,128)S(1)}, u32[]{:S(2)}, u32[]{:S(2)}) %collective-permute-start.4) | collective-permute-done | bytes 110624 | tf_op jit(solution)/shard_map/ppermute | solution.py:14
  59.4 1.3 %collective-permute-start.5 = (f32[3,24,384]{2,1,0:T(8,128)S(1)}, f32[3,24,384]{2,1,0:T(8,128)S(1)}, u32[]{:S(2)}, u32[]{:S(2)}) collective-permute-start(f32[3,24,384]{2,1,0:T(8,128)S(1)} %get-tuple-element.122), channel_id=1, source_target_pairs={{1,0},{3,2},{5,4},{7,6},{9,8},{11,10},{13,12},{15,14},{17,16},{19,... | collective-permute-start | bytes 331784 | tf_op jit(solution)/shard_map/ppermute | solution.py:15
  60.7 5.3 %collective-permute-done.5 = f32[3,24,384]{2,1,0:T(8,128)S(1)} collective-permute-done((f32[3,24,384]{2,1,0:T(8,128)S(1)}, f32[3,24,384]{2,1,0:T(8,128)S(1)}, u32[]{:S(2)}, u32[]{:S(2)}) %collective-permute-start.5) | collective-permute-done | bytes 110624 | tf_op jit(solution)/shard_map/ppermute | solution.py:15
  66.0 1.6 %fusion.226 = f32[4,24,384]{2,1,0:T(8,128)} fusion(f32[4,24,384]{2,1,0:T(8,128)} %copy-done.1, f32[3,24,384]{2,1,0:T(8,128)S(1)} %collective-permute-done.5), kind=kLoop, calls=%fused_computation.310 | loop fusion | flops 27648 | bytes 331776 | tf_op jit(solution)/shard_map/scatter-add | solution.py:83
  (89 shorter events, 7.8 us)
Async XLA Ops:
  10.7 7.8 %collective-permute-start = (f32[1,4,1,128]{3,2,1,0:T(1,128)S(1)}, f32[1,4,1,128]{3,2,1,0:T(1,128)S(1)}, u32[]{:S(2)}, u32[]{:S(2)}) collective-permute-start(f32[1,4,1,128]{3,2,1,0:T(1,128)S(1)} %slice.470), channel_id=1, source_target_pairs={{2,0},{4,2},{6,4},{8,6},{10,8},{12,10},{14,12},{16,14},{18,16},{20... | collective-permute-start | bytes 6152 | tf_op jit(solution)/shard_map/ppermute | solution.py:23
  15.0 10.1 %all-to-all-start.2 = ((f32[16,1,512]{2,1,0:T(1,128)}), f32[16,1,512]{2,1,0:T(1,128)S(1)}, u32[]{:S(2)}, u32[]{:S(2)}) async-start(f32[16,1,512]{2,1,0:T(1,128)} %reshape.851), calls=%async_computation.2 | async-start | bytes 65536 | tf_op jit(solution)/shard_map/all_to_all | solution.py:99
  18.9 1.0 %copy-start = (f32[4,24,384]{2,1,0:T(8,128)S(1)}, f32[4,24,384]{2,1,0:T(8,128)}, u32[]{:S(2)}) copy-start(f32[4,24,384]{2,1,0:T(8,128)} %param.20) | copy-start | bytes 442372
  25.1 23.6 %all-to-all-start.1 = ((f32[16,1,2304]{2,1,0:T(1,128)}), f32[16,1,2304]{2,1,0:T(1,128)S(1)}, u32[]{:S(2)}, u32[]{:S(2)}) async-start(f32[16,1,2304]{2,1,0:T(1,128)} %reshape.849), calls=%async_computation.1 | async-start | bytes 294912 | tf_op jit(solution)/shard_map/all_to_all | solution.py:97
  33.8 6.5 %collective-permute-start.1 = (f32[2,4,1,384]{3,1,2,0:T(4,128)S(1)}, f32[2,4,1,384]{3,1,2,0:T(4,128)S(1)}, u32[]{:S(2)}, u32[]{:S(2)}) collective-permute-start(f32[2,4,1,384]{3,1,2,0:T(4,128)S(1)} %copy.366), channel_id=1, source_target_pairs={{2,0},{4,2},{6,4},{8,6},{10,8},{12,10},{14,12},{16,14},{18,16},{20... | collective-permute-start | bytes 36872 | tf_op jit(solution)/shard_map/ppermute | solution.py:23
  40.5 4.2 %collective-permute-start.3 = (f32[1,24,384]{2,0,1:T(1,128)S(1)}, f32[1,24,384]{2,0,1:T(1,128)S(1)}, u32[]{:S(2)}, u32[]{:S(2)}) collective-permute-start(f32[1,24,384]{2,0,1:T(1,128)S(1)} %bitcast.97), channel_id=1, source_target_pairs={{0,1},{2,3},{4,5},{6,7},{8,9},{10,11},{12,13},{14,15},{16,17},{18,... | collective-permute-start | bytes 110600 | tf_op jit(solution)/shard_map/ppermute | solution.py:14
  42.8 5.9 %collective-permute-start.2 = (f32[1,24,384]{2,0,1:T(1,128)S(1)}, f32[1,24,384]{2,0,1:T(1,128)S(1)}, u32[]{:S(2)}, u32[]{:S(2)}) collective-permute-start(f32[1,24,384]{2,0,1:T(1,128)S(1)} %bitcast.98), channel_id=1, source_target_pairs={{1,0},{3,2},{5,4},{7,6},{9,8},{11,10},{13,12},{15,14},{17,16},{19,... | collective-permute-start | bytes 110600 | tf_op jit(solution)/shard_map/ppermute | solution.py:15
  55.4 3.9 %collective-permute-start.4 = (f32[3,24,384]{2,1,0:T(8,128)S(1)}, f32[3,24,384]{2,1,0:T(8,128)S(1)}, u32[]{:S(2)}, u32[]{:S(2)}) collective-permute-start(f32[3,24,384]{2,1,0:T(8,128)S(1)} %slice.519), channel_id=1, source_target_pairs={{0,1},{2,3},{4,5},{6,7},{8,9},{10,11},{12,13},{14,15},{16,17},{18,... | collective-permute-start | bytes 331784 | tf_op jit(solution)/shard_map/ppermute | solution.py:14
  59.4 6.7 %copy-start.1 = (f32[4,24,384]{2,1,0:T(8,128)}, f32[4,24,384]{2,1,0:T(8,128)S(1)}, u32[]{:S(2)}) copy-start(f32[4,24,384]{2,1,0:T(8,128)S(1)} %get-tuple-element.123) | copy-start | bytes 442372
  59.4 6.6 %collective-permute-start.5 = (f32[3,24,384]{2,1,0:T(8,128)S(1)}, f32[3,24,384]{2,1,0:T(8,128)S(1)}, u32[]{:S(2)}, u32[]{:S(2)}) collective-permute-start(f32[3,24,384]{2,1,0:T(8,128)S(1)} %get-tuple-element.122), channel_id=1, source_target_pairs={{1,0},{3,2},{5,4},{7,6},{9,8},{11,10},{13,12},{15,14},{17,16},{19,... | collective-permute-start | bytes 331784 | tf_op jit(solution)/shard_map/ppermute | solution.py:15
where the time goes:
time: 68 us; the launch traced here: 67.6 us
  starting transfers between devices  22.1 us (32%)
  local copies, waits for them, and re-layouts  15.1 us (22%)
  waiting for transfers between devices  12.6 us (19%)
  other arithmetic  9.22 us (14%)
  blocking collectives  8.07 us (12%)
    ppermute x2, waiting for transfers between devices, padded_2(): after = lax.ppermute(initial, axis, down)  9.27 us
    all_to_all x1, blocking collectives, local(): lax.all_to_all(velocity, 'gz', split_axis=1, concat_axis=3, tiled=True)  8.07 us
    ppermute x2, starting transfers between devices, passed_along(): return lax.ppermute(block, axis, route)  7.05 us
    unnamed x15, local copies, waits for them, and re-layouts  5.7 us
    all_to_all x1, starting transfers between devices, local(): lax.all_to_all(turned, 'gy', split_axis=1, concat_axis=2, tiled=True)  4.95 us
    ppermute x2, starting transfers between devices, padded_2(): before = lax.ppermute(last, axis, up)  3.81 us
    all_to_all x1, starting transfers between devices, local(): lax.all_to_all(coarse_rows, 'gy', split_axis=2, concat_axis=3, tiled=True)  3.49 us
    ppermute x2, starting transfers between devices, padded_2(): after = lax.ppermute(initial, axis, down)  2.76 us
  transfers between devices with their start and end apart: 8, of which 4 were waited for; matrix products, arithmetic and copies ran while one was open for 19% of the time, Pallas kernels for 0%

commit v1 on v0

--- a/solution.py
+++ b/solution.py
@@ -96,7 +96,10 @@
     sending = coarse[1:]
     field = lax.all_to_all(turned, "gy", split_axis=1, concat_axis=2, tiled=True)
     coarse_rows = jnp.swapaxes(sending, 2, 3)
-    coarse_turned = lax.all_to_all(coarse_rows, "gy", split_axis=2, concat_axis=3, tiled=True)
+    coarse_turned = jnp.concatenate(
+        lax.all_to_all(jnp.stack(jnp.split(coarse_rows, lax.axis_size("gy"), axis=2)), "gy", 0, 0),
+        axis=3,
+    )
     y_refined = alternate(coarse_turned, jnp.roll(coarse_turned, -1, 3), 3)
     next_col = passed_along(y_refined[:, :, :1, :], "gy", -1)
     pencil_vel = alternate(

time: 68 us -> 68.4 us (level)
    reshape x0 -> x4, local copies, waits for them, and re-layouts: none -> 0.82 us  [local(): jnp.concatenate(lax.all_to_all(jnp.stack(jnp.split(coarse_rows, lax.axis_...]
    all_to_all x3 -> x0, local copies, waits for them, and re-layouts: 0.81 us -> none  [local(): lax.all_to_all(coarse_rows, 'gy', split_axis=2, concat_axis=3, tiled=True)]
    unnamed x15 -> x30, local copies, waits for them, and re-layouts: 5.7 us -> 6.19 us
  transfers between devices with their start and end apart: 8 -> 8, of which waited for: 4 -> 4; matrix products, arithmetic and copies ran while one was open for 19% -> 18% of each run, Pallas kernels for 0% -> 0%
where the time goes in v1:
time: 68.4 us; the launch traced here: 67.9 us
  starting transfers between devices  22.1 us (32%)
  local copies, waits for them, and re-layouts  15.4 us (23%)
  waiting for transfers between devices  12.6 us (18%)
  other arithmetic  9.22 us (13%)
  blocking collectives  8.07 us (12%)
    ppermute x2, waiting for transfers between devices, padded_2(): after = lax.ppermute(initial, axis, down)  9.27 us
    all_to_all x1, blocking collectives, local(): lax.all_to_all(velocity, 'gz', split_axis=1, concat_axis=3, tiled=True)  8.07 us
    ppermute x2, starting transfers between devices, passed_along(): return lax.ppermute(block, axis, route)  7.05 us
    unnamed x30, local copies, waits for them, and re-layouts  6.19 us
    all_to_all x1, starting transfers between devices, local(): lax.all_to_all(turned, 'gy', split_axis=1, concat_axis=2, tiled=True)  4.95 us
    ppermute x2, starting transfers between devices, padded_2(): before = lax.ppermute(last, axis, up)  3.81 us
    all_to_all x1, starting transfers between devices, local(): lax.all_to_all(jnp.stack(jnp.split(coarse_rows, lax.axis_size('gy'), axis...  3.49 us
    ppermute x2, starting transfers between devices, padded_2(): after = lax.ppermute(initial, axis, down)  2.76 us
  transfers between devices with their start and end apart: 8, of which 4 were waited for; matrix products, arithmetic and copies ran while one was open for 18% of the time, Pallas kernels for 0%

profile of v1, /device:TPU:0, one launch (start us, length us, event | category | flops | bytes accessed | tf_op | source)
XLA Modules:
  0.0 67.9 jit_solution(13473637090510232205)
XLA Ops:
  0.0 0.9 %copy.393 = f32[3,8,8,64]{3,2,0,1:T(8,128)S(1)} copy(f32[3,8,8,64]{3,2,1,0:T(8,128)} %param.21) | data formatting | bytes 98304 | tf_op args[1]
  1.0 8.1 %all_to_all.38 = f32[2,1,6144]{2,1,0:T(1,128)S(1)} all-to-all(f32[2,1,6144]{2,1,0:T(1,128)S(1)} %reshape.858), channel_id=1, replica_groups=mesh['gy'=16,'gz'=2] {'gz'}, dimensions={0} | all-to-all | bytes 98304 | tf_op jit(solution)/shard_map/all_to_all | solution.py:88
  9.1 0.5 broadcast.909
  9.6 0.8 %reduce.18 = f32[2,6144]{1,0:T(2,128)S(1)} reduce(f32[2,1,6144]{2,1,0:T(1,128)S(1)} %all_to_all.38, f32[]{:T(128)} %broadcast.909), dimensions={1}, to_apply=%all_to_all.27.reduce_sub_computation | reduce | bytes 98308 | tf_op jit(solution)/shard_map/all_to_all | solution.py:88
  12.0 2.7 %collective-permute-start = (f32[1,4,1,128]{3,2,1,0:T(1,128)S(1)}, f32[1,4,1,128]{3,2,1,0:T(1,128)S(1)}, u32[]{:S(2)}, u32[]{:S(2)}) collective-permute-start(f32[1,4,1,128]{3,2,1,0:T(1,128)S(1)} %slice.470), channel_id=1, source_target_pairs={{2,0},{4,2},{6,4},{8,6},{10,8},{12,10},{14,12},{16,14},{18,16},{20... | collective-permute-start | bytes 6152 | tf_op jit(solution)/shard_map/ppermute | solution.py:23
  14.8 0.9 %reshape.862 = f32[16,1,512]{2,1,0:T(1,128)} reshape(f32[16,2,4,8,8]{4,3,2,1,0:T(8,128)S(1)} %bitcast.165) | data formatting | bytes 65536
  15.7 3.5 %all-to-all-start.2 = ((f32[16,1,512]{2,1,0:T(1,128)}), f32[16,1,512]{2,1,0:T(1,128)S(1)}, u32[]{:S(2)}, u32[]{:S(2)}) async-start(f32[16,1,512]{2,1,0:T(1,128)} %reshape.862), calls=%async_computation.2 | async-start | bytes 65536 | tf_op jit(solution)/shard_map/all_to_all | solution.py:100
  20.8 1.0 %fusion.22 = (f32[4,24,384]{2,1,0:T(8,128)S(1)}, f32[4,24,384]{2,1,0:T(8,128)S(1)}, f32[4,24,384]{2,1,0:T(8,128)S(1)}, f32[4,24,384]{2,1,0:T(8,128)S(1)}, f32[4,24,384]{2,1,0:T(8,128)S(1)}) fusion(f32[4,24,384]{2,1,0:T(8,128)S(1)} %copy-done, f32[4,24,384]{2,1,0:T(8,128)S(1)} %get-tuple-element.121), kind=kLoop, calls=%fused_computation.46 | loop fusion | flops 7741440 | bytes 1032192 | tf_op jit(solution)/shard_map/mul | solution.py:68
  23.1 1.7 %reshape.860 = f32[16,1,2304]{2,1,0:T(1,128)} reshape(f32[384,4,24]{2,1,0:T(4,128)S(1)} %bitcast.154) | data formatting | bytes 294912
  24.7 1.0 %all-to-all-done.2 = f32[16,1,512]{2,1,0:T(1,128)S(1)} async-done(((f32[16,1,512]{2,1,0:T(1,128)}), f32[16,1,512]{2,1,0:T(1,128)S(1)}, u32[]{:S(2)}, u32[]{:S(2)}) %all-to-all-start.2) | async-done | bytes 32800 | tf_op jit(solution)/shard_map/all_to_all | solution.py:100
  25.8 4.9 %all-to-all-start.1 = ((f32[16,1,2304]{2,1,0:T(1,128)}), f32[16,1,2304]{2,1,0:T(1,128)S(1)}, u32[]{:S(2)}, u32[]{:S(2)}) async-start(f32[16,1,2304]{2,1,0:T(1,128)} %reshape.860), calls=%async_computation.1 | async-start | bytes 294912 | tf_op jit(solution)/shard_map/all_to_all | solution.py:97
  30.7 0.7 %reduce.19 = f32[16,512]{1,0:T(8,128)S(1)} reduce(f32[16,1,512]{2,1,0:T(1,128)S(1)} %all-to-all-done.2, f32[]{:T(128)} %broadcast.909), dimensions={1}, to_apply=%all_to_all.34.reduce_sub_computation | reduce | bytes 65540 | tf_op jit(solution)/shard_map/all_to_all | solution.py:100
  32.8 0.7 %copy.356 = f32[2,4,8,128,3]{2,1,4,3,0:T(4,128)S(1)} copy(f32[2,4,8,128,3]{3,2,1,0,4:T(8,128)S(1)} %pad_maximum_fusion.4) | data formatting | bytes 196608 | tf_op jit(solution)/shard_map/stack | solution.py:28
  33.5 0.6 copy.358
  34.1 4.4 %collective-permute-start.1 = (f32[2,4,1,384]{3,1,2,0:T(4,128)S(1)}, f32[2,4,1,384]{3,1,2,0:T(4,128)S(1)}, u32[]{:S(2)}, u32[]{:S(2)}) collective-permute-start(f32[2,4,1,384]{3,1,2,0:T(4,128)S(1)} %copy.358), channel_id=1, source_target_pairs={{2,0},{4,2},{6,4},{8,6},{10,8},{12,10},{14,12},{16,14},{18,16},{20... | collective-permute-start | bytes 36872 | tf_op jit(solution)/shard_map/ppermute | solution.py:23
  38.5 0.9 %slice_bitcast_fusion = f32[2,4,7,1,384]{2,1,4,0,3:T(4,128)S(1)} fusion(f32[2,4,8,384]{2,1,3,0:T(4,128)S(1)} %bitcast.132), kind=kLoop, calls=%fused_computation | loop fusion | bytes 172032 | tf_op jit(solution)/shard_map/concatenate | solution.py:106
  39.4 0.6 copy.361
  40.0 0.7 copy.359
  40.9 2.2 %collective-permute-start.3 = (f32[1,24,384]{2,0,1:T(1,128)S(1)}, f32[1,24,384]{2,0,1:T(1,128)S(1)}, u32[]{:S(2)}, u32[]{:S(2)}) collective-permute-start(f32[1,24,384]{2,0,1:T(1,128)S(1)} %bitcast.171), channel_id=1, source_target_pairs={{0,1},{2,3},{4,5},{6,7},{8,9},{10,11},{12,13},{14,15},{16,17},{18,... | collective-permute-start | bytes 110600 | tf_op jit(solution)/shard_map/ppermute | solution.py:14
  43.1 1.5 %collective-permute-start.2 = (f32[1,24,384]{2,0,1:T(1,128)S(1)}, f32[1,24,384]{2,0,1:T(1,128)S(1)}, u32[]{:S(2)}, u32[]{:S(2)}) collective-permute-start(f32[1,24,384]{2,0,1:T(1,128)S(1)} %bitcast.172), channel_id=1, source_target_pairs={{1,0},{3,2},{5,4},{7,6},{9,8},{11,10},{13,12},{15,14},{17,16},{19,... | collective-permute-start | bytes 110600 | tf_op jit(solution)/shard_map/ppermute | solution.py:15
  45.0 3.9 %collective-permute-done.2 = f32[1,24,384]{2,0,1:T(1,128)S(1)} collective-permute-done((f32[1,24,384]{2,0,1:T(1,128)S(1)}, f32[1,24,384]{2,0,1:T(1,128)S(1)}, u32[]{:S(2)}, u32[]{:S(2)}) %collective-permute-start.2) | collective-permute-done | bytes 36896 | tf_op jit(solution)/shard_map/ppermute | solution.py:15
  49.0 1.0 %reduce.20 = f32[16,2304]{1,0:T(8,128)S(1)} reduce(f32[16,1,2304]{2,1,0:T(1,128)S(1)} %all-to-all-done.1, f32[]{:T(128)} %broadcast.909), dimensions={1}, to_apply=%all_to_all.30.reduce_sub_computation | reduce | bytes 294916 | tf_op jit(solution)/shard_map/all_to_all | solution.py:97
  50.0 1.1 %reshape.861 = f32[384,4,24]{2,1,0:T(4,128)S(1)} reshape(f32[16,2304]{1,0:T(8,128)S(1)} %reduce.20) | data formatting | bytes 294912
  51.0 0.5 copy.391
  51.5 0.4 all_to_all.33
  52.2 1.0 %fusion.28 = (f32[4,24,384]{2,1,0:T(8,128)S(1)}, f32[4,24,384]{2,1,0:T(8,128)S(1)}, f32[4,24,384]{2,1,0:T(8,128)S(1)}, f32[4,24,384]{2,1,0:T(8,128)S(1)}, f32[4,24,384]{2,1,0:T(8,128)S(1)}) fusion(f32[4,24,384]{2,1,0:T(8,128)S(1)} %all_to_all.33, f32[4,24,384]{2,1,0:T(8,128)S(1)} %get-tuple-element.119), kind=kLoop, calls=%fused_computation.52 | loop fusion | flops 7741440 | bytes 1032192 | tf_op jit(solution)/shard_map/mul | solution.py:68
  53.8 0.6 fusion.53
  55.8 1.6 %collective-permute-start.4 = (f32[3,24,384]{2,1,0:T(8,128)S(1)}, f32[3,24,384]{2,1,0:T(8,128)S(1)}, u32[]{:S(2)}, u32[]{:S(2)}) collective-permute-start(f32[3,24,384]{2,1,0:T(8,128)S(1)} %slice.519), channel_id=1, source_target_pairs={{0,1},{2,3},{4,5},{6,7},{8,9},{10,11},{12,13},{14,15},{16,17},{18,... | collective-permute-start | bytes 331784 | tf_op jit(solution)/shard_map/ppermute | solution.py:14
  57.4 2.3 %collective-permute-done.4 = f32[3,24,384]{2,1,0:T(8,128)S(1)} collective-permute-done((f32[3,24,384]{2,1,0:T(8,128)S(1)}, f32[3,24,384]{2,1,0:T(8,128)S(1)}, u32[]{:S(2)}, u32[]{:S(2)}) %collective-permute-start.4) | collective-permute-done | bytes 110624 | tf_op jit(solution)/shard_map/ppermute | solution.py:14
  59.7 1.3 %collective-permute-start.5 = (f32[3,24,384]{2,1,0:T(8,128)S(1)}, f32[3,24,384]{2,1,0:T(8,128)S(1)}, u32[]{:S(2)}, u32[]{:S(2)}) collective-permute-start(f32[3,24,384]{2,1,0:T(8,128)S(1)} %get-tuple-element.122), channel_id=1, source_target_pairs={{1,0},{3,2},{5,4},{7,6},{9,8},{11,10},{13,12},{15,14},{17,16},{19,... | collective-permute-start | bytes 331784 | tf_op jit(solution)/shard_map/ppermute | solution.py:15
  61.0 5.3 %collective-permute-done.5 = f32[3,24,384]{2,1,0:T(8,128)S(1)} collective-permute-done((f32[3,24,384]{2,1,0:T(8,128)S(1)}, f32[3,24,384]{2,1,0:T(8,128)S(1)}, u32[]{:S(2)}, u32[]{:S(2)}) %collective-permute-start.5) | collective-permute-done | bytes 110624 | tf_op jit(solution)/shard_map/ppermute | solution.py:15
  66.4 1.6 %fusion.226 = f32[4,24,384]{2,1,0:T(8,128)} fusion(f32[4,24,384]{2,1,0:T(8,128)} %copy-done.1, f32[3,24,384]{2,1,0:T(8,128)S(1)} %collective-permute-done.5), kind=kLoop, calls=%fused_computation.309 | loop fusion | flops 27648 | bytes 331776 | tf_op jit(solution)/shard_map/scatter-add | solution.py:83
  (105 shorter events, 8.6 us)
Async XLA Ops:
  12.0 7.2 %collective-permute-start = (f32[1,4,1,128]{3,2,1,0:T(1,128)S(1)}, f32[1,4,1,128]{3,2,1,0:T(1,128)S(1)}, u32[]{:S(2)}, u32[]{:S(2)}) collective-permute-start(f32[1,4,1,128]{3,2,1,0:T(1,128)S(1)} %slice.470), channel_id=1, source_target_pairs={{2,0},{4,2},{6,4},{8,6},{10,8},{12,10},{14,12},{16,14},{18,16},{20... | collective-permute-start | bytes 6152 | tf_op jit(solution)/shard_map/ppermute | solution.py:23
  15.7 10.1 %all-to-all-start.2 = ((f32[16,1,512]{2,1,0:T(1,128)}), f32[16,1,512]{2,1,0:T(1,128)S(1)}, u32[]{:S(2)}, u32[]{:S(2)}) async-start(f32[16,1,512]{2,1,0:T(1,128)} %reshape.862), calls=%async_computation.2 | async-start | bytes 65536 | tf_op jit(solution)/shard_map/all_to_all | solution.py:100
  19.5 1.0 %copy-start = (f32[4,24,384]{2,1,0:T(8,128)S(1)}, f32[4,24,384]{2,1,0:T(8,128)}, u32[]{:S(2)}) copy-start(f32[4,24,384]{2,1,0:T(8,128)} %param.20) | copy-start | bytes 442372
  25.8 23.2 %all-to-all-start.1 = ((f32[16,1,2304]{2,1,0:T(1,128)}), f32[16,1,2304]{2,1,0:T(1,128)S(1)}, u32[]{:S(2)}, u32[]{:S(2)}) async-start(f32[16,1,2304]{2,1,0:T(1,128)} %reshape.860), calls=%async_computation.1 | async-start | bytes 294912 | tf_op jit(solution)/shard_map/all_to_all | solution.py:97
  34.1 6.5 %collective-permute-start.1 = (f32[2,4,1,384]{3,1,2,0:T(4,128)S(1)}, f32[2,4,1,384]{3,1,2,0:T(4,128)S(1)}, u32[]{:S(2)}, u32[]{:S(2)}) collective-permute-start(f32[2,4,1,384]{3,1,2,0:T(4,128)S(1)} %copy.358), channel_id=1, source_target_pairs={{2,0},{4,2},{6,4},{8,6},{10,8},{12,10},{14,12},{16,14},{18,16},{20... | collective-permute-start | bytes 36872 | tf_op jit(solution)/shard_map/ppermute | solution.py:23
  40.9 4.2 %collective-permute-start.3 = (f32[1,24,384]{2,0,1:T(1,128)S(1)}, f32[1,24,384]{2,0,1:T(1,128)S(1)}, u32[]{:S(2)}, u32[]{:S(2)}) collective-permute-start(f32[1,24,384]{2,0,1:T(1,128)S(1)} %bitcast.171), channel_id=1, source_target_pairs={{0,1},{2,3},{4,5},{6,7},{8,9},{10,11},{12,13},{14,15},{16,17},{18,... | collective-permute-start | bytes 110600 | tf_op jit(solution)/shard_map/ppermute | solution.py:14
  43.1 5.9 %collective-permute-start.2 = (f32[1,24,384]{2,0,1:T(1,128)S(1)}, f32[1,24,384]{2,0,1:T(1,128)S(1)}, u32[]{:S(2)}, u32[]{:S(2)}) collective-permute-start(f32[1,24,384]{2,0,1:T(1,128)S(1)} %bitcast.172), channel_id=1, source_target_pairs={{1,0},{3,2},{5,4},{7,6},{9,8},{11,10},{13,12},{15,14},{17,16},{19,... | collective-permute-start | bytes 110600 | tf_op jit(solution)/shard_map/ppermute | solution.py:15
  55.8 3.9 %collective-permute-start.4 = (f32[3,24,384]{2,1,0:T(8,128)S(1)}, f32[3,24,384]{2,1,0:T(8,128)S(1)}, u32[]{:S(2)}, u32[]{:S(2)}) collective-permute-start(f32[3,24,384]{2,1,0:T(8,128)S(1)} %slice.519), channel_id=1, source_target_pairs={{0,1},{2,3},{4,5},{6,7},{8,9},{10,11},{12,13},{14,15},{16,17},{18,... | collective-permute-start | bytes 331784 | tf_op jit(solution)/shard_map/ppermute | solution.py:14
  59.7 6.7 %copy-start.1 = (f32[4,24,384]{2,1,0:T(8,128)}, f32[4,24,384]{2,1,0:T(8,128)S(1)}, u32[]{:S(2)}) copy-start(f32[4,24,384]{2,1,0:T(8,128)S(1)} %get-tuple-element.123) | copy-start | bytes 442372
  59.7 6.6 %collective-permute-start.5 = (f32[3,24,384]{2,1,0:T(8,128)S(1)}, f32[3,24,384]{2,1,0:T(8,128)S(1)}, u32[]{:S(2)}, u32[]{:S(2)}) collective-permute-start(f32[3,24,384]{2,1,0:T(8,128)S(1)} %get-tuple-element.122), channel_id=1, source_target_pairs={{1,0},{3,2},{5,4},{7,6},{9,8},{11,10},{13,12},{15,14},{17,16},{19,... | collective-permute-start | bytes 331784 | tf_op jit(solution)/shard_map/ppermute | solution.py:15
